TPU v7x, 32 devices: a whole 2x2x4 slice. The times are simulated.
32 devices in a mesh: groups: 2 (over y), dp: 4 (over z), tensor: 4 (over x, core).
Axes of the slice: x: 2, y: 2, z: 4, core: 2. Of those that a mesh axis runs over, the one named last changes fastest.
Arguments:
- patches: bfloat16 [8192, 1280], P(('groups', 'dp')), parts along dimension 0, may hold values from -64 to 64
- grids: int32 [8, 2], P(('groups', 'dp')), parts along dimension 0, may hold values from 16 to 32, as said below
- dest: int32 [8, 256], P(('groups', 'dp')), parts along dimension 0, may hold values from 0 to 1535, as said below
- norm_gain: float32 [1280], replicated, may hold values from 0.1 to 1.9
- qkv_weight: bfloat16 [3, 1280, 1280], P(None, None, 'tensor'), may hold values from -8 to 8
- qkv_bias: float32 [3, 1280], P(None, 'tensor'), may hold values from -3 to 3
- proj_weight: bfloat16 [1280, 1280], P('tensor'), may hold values from -0.15625 to 0.15625
- proj_bias: float32 [1280], replicated, may hold values from -3 to 3
- merge_gain: float32 [1280], replicated, may hold values from 0.1 to 1.9
- w_first: bfloat16 [5120, 5120], P('dp', 'tensor'), may hold values from -0.078125 to 0.078125
- b_first: float32 [5120], P('tensor'), may hold values from -3 to 3
- w_second: bfloat16 [5120, 8192], P('tensor', 'dp'), may hold values from -0.078125 to 0.078125
- b_second: float32 [8192], P('tensor'), may hold values from -3 to 3
- text_embed: bfloat16 [3072, 8192], P(('groups', 'dp'), 'tensor'), parts along dimension 0, may hold values from -6 to 6
Outputs:
- sequence: bfloat16 [3072, 8192], P(('groups', 'dp'), 'tensor'), parts along dimension 0
There are 2 independent parts, one for each index of `groups`. A program takes and returns all parts, laid end to end along the dimension named above; an argument that names none is the same for every part. Nothing has to cross between parts.
Inputs may be any that keep to these rules, and one draw needn't show every extreme that they name: `grids`: both sides of every grid are even, at least 16 and at most 32; in each part along `groups`, the first image (the one on dp index 0) has the full 32 x 32 grid. The rows dest[i, j] with j < grids[i, 0] * grids[i, 1] / 4 are distinct over all images; the live rows of one image reach at most 64 rows in each aligned block of 384 sequence rows, and exactly that many for a full grid.
All inputs are finite; a program needn't handle non-finite values.
Results may differ from a plain program's by a relative error of at most 0.014.
Values may be sent and summed in bfloat16 or wider, within the bound.
A program may use at most 128 MiB of HBM per device.

v0:
```python
import math

import jax
import jax.numpy as jnp
from jax import lax
from jax.sharding import PartitionSpec as P

HEAD_DIM = 80
PATCHES = 1024
MERGED = 256


def rms_scale(values, gain):
    return values * lax.rsqrt(jnp.mean(values * values, axis=-1, keepdims=True) + 1e-06) * gain


def local(
    patches,
    grids,
    dest,
    norm_gain,
    qkv_weight,
    qkv_bias,
    proj_weight,
    proj_bias,
    merge_gain,
    w_first,
    b_first,
    w_second,
    b_second,
    text_embed,
):
    rows_dev = patches.shape[0]
    images_dev = grids.shape[0]
    heads_dev = qkv_weight.shape[2] // HEAD_DIM
    live_count = grids[:, 0] * grids[:, 1]
    normed = rms_scale(patches.astype(jnp.float32), norm_gain).astype(jnp.bfloat16)
    projected = (
        jnp.einsum("rv,jvc->jrc", normed, qkv_weight, preferred_element_type=jnp.float32)
        + qkv_bias[:, None, :]
    )
    projected = projected.astype(jnp.bfloat16).reshape(3, images_dev, PATCHES, heads_dev, HEAD_DIM)
    scores = jnp.einsum(
        "iqhd,ikhd->ihqk", projected[0], projected[1], preferred_element_type=jnp.float32
    ) / math.sqrt(HEAD_DIM)
    live_keys = jnp.arange(PATCHES, dtype=jnp.int32)[None, :] < live_count[:, None]
    scores = jnp.where(live_keys[:, None, None, :], scores, jnp.float32(-1e30))
    peak_score = jnp.max(scores, axis=-1, keepdims=True)
    exponent = jnp.exp(scores - peak_score)
    weights = (exponent / jnp.sum(exponent, axis=-1, keepdims=True)).astype(jnp.bfloat16)
    attended = jnp.einsum(
        "ihqk,ikhd->iqhd", weights, projected[2], preferred_element_type=jnp.float32
    )
    attended = attended.astype(jnp.bfloat16).reshape(rows_dev, heads_dev * HEAD_DIM)
    partial_value = jnp.dot(attended, proj_weight, preferred_element_type=jnp.float32).astype(
        jnp.bfloat16
    )
    summed = lax.psum(partial_value, "tensor").astype(jnp.float32)
    resid = patches.astype(jnp.float32) + summed + proj_bias
    merged_in = rms_scale(resid, merge_gain).astype(jnp.bfloat16)
    merged_in = merged_in.reshape(rows_dev // 4, 4 * patches.shape[1])
    merged_dev = merged_in.shape[0]
    received = lax.all_to_all(merged_in, "dp", split_axis=1, concat_axis=0, tiled=True)
    first_out = lax.psum_scatter(
        jnp.dot(received, w_first, preferred_element_type=jnp.float32).astype(jnp.bfloat16),
        "dp",
        scatter_dimension=0,
        tiled=True,
    ).astype(jnp.float32)
    hidden = jax.nn.gelu(first_out + b_first, approximate=False).astype(jnp.bfloat16)
    second_rows = jnp.dot(
        hidden,
        lax.all_gather(w_second, "dp", axis=1, tiled=True),
        preferred_element_type=jnp.float32,
    ).astype(jnp.bfloat16)
    visual = lax.psum_scatter(second_rows, "tensor", scatter_dimension=1, tiled=True).astype(
        jnp.float32
    )
    visual = (visual + b_second).astype(jnp.bfloat16)
    feature_count = visual.shape[1]
    dp_count = lax.axis_size("dp")
    seq_rows = text_embed.shape[0]
    capacity = images_dev * (MERGED // dp_count)
    live_rows = (jnp.arange(MERGED, dtype=jnp.int32)[None, :] < (live_count // 4)[:, None]).reshape(
        merged_dev
    )
    dest_flat = dest.reshape(merged_dev)
    shard_id = jnp.where(live_rows, dest_flat // seq_rows, dp_count)
    local_row = dest_flat % seq_rows
    one_hot = (shard_id[:, None] == jnp.arange(dp_count, dtype=jnp.int32)[None, :]).astype(
        jnp.int32
    )
    before = jnp.cumsum(one_hot, axis=0) - one_hot
    slot_index = jnp.sum(before * one_hot, axis=1)
    buffer = (
        jnp.zeros((dp_count, capacity, feature_count), jnp.bfloat16)
        .at[shard_id, slot_index]
        .set(visual, mode="drop")
    )
    positions = (
        jnp.full((dp_count, capacity), seq_rows, jnp.int32)
        .at[shard_id, slot_index]
        .set(local_row, mode="drop")
    )
    arrived, arrived_rows = (
        lax.all_to_all(buffer, "dp", split_axis=0, concat_axis=0, tiled=True),
        lax.all_to_all(positions, "dp", split_axis=0, concat_axis=0, tiled=True),
    )
    sequence = text_embed.at[arrived_rows.reshape(-1)].set(
        arrived.reshape(-1, feature_count), mode="drop"
    )
    return sequence


def solution(mesh):
    in_specs = (
        P(("groups", "dp"), None),
        P(("groups", "dp"), None),
        P(("groups", "dp"), None),
        P(),
        P(None, None, "tensor"),
        P(None, "tensor"),
        P("tensor", None),
        P(),
        P(),
        P("dp", "tensor"),
        P("tensor"),
        P("tensor", "dp"),
        P("tensor"),
        P(("groups", "dp"), "tensor"),
    )
    out_specs = P(("groups", "dp"), "tensor")
    return jax.shard_map(local, mesh=mesh, in_specs=in_specs, out_specs=out_specs, check_vma=False)
```

profile of v0, /device:TPU:0, one launch (start us, length us, event | category | flops | bytes accessed | tf_op | source)
XLA Modules:
  0.0 748.9 jit_solution(11529100986900097305)
XLA Ops:
  6.5 2.9 copy.35
  13.1 2.9 fusion.15
  15.9 1.3 fusion.103
  17.3 10.9 %fusion.105 = (f32[4,1024]{1,0:T(4,128)S(1)}, f32[4,1024,1024]{1,2,0:T(8,128)}) fusion(pred[1024]{0:T(1024)(128)(4,1)S(1)} %iota_compare_fusion, bf16[1024,4,80]{0,2,1:T(8,128)(2,1)} %bitcast.76, bf16[1024,4,80]{0,2,1:T(8,128)(2,1)} %bitcast.75), kind=kOutput, calls=%fused_computation.150 | convolution fusion | flops 687866880 | bytes 18105344 | tf_op jit(solution)/shard_map/sub | solution.py:49
  28.1 7.6 %fusion.20 = bf16[4,80,1024]{2,1,0:T(8,128)(2,1)S(1)} fusion(bf16[1024,4,80]{0,2,1:T(8,128)(2,1)} %bitcast.74, f32[4,1024,1024]{1,2,0:T(8,128)} %get-tuple-element.17, f32[4,1024]{1,0:T(4,128)S(1)} %get-tuple-element.16), kind=kOutput, calls=%fused_computation.33 | convolution fusion | flops 679804928 | bytes 18104320 | tf_op jit(solution)/shard_map/ihqk,ikhd->iqhd/dot_general | solution.py:51
  35.8 3.1 convolution_convert_fusion.2
  39.1 62.5 %all-reduce.2.cloned.1.call-done = bf16[1024,1280]{1,0:T(8,128)(2,1)} async-done(((bf16[1024,1280]{1,0:T(8,128)(2,1)}), bf16[1024,1280]{1,0:T(8,128)(2,1)}) %all-reduce.2.cloned.1.call-update) | async-done | bytes 2621456 | tf_op jit(solution)/shard_map/psum | solution.py:58
  101.7 3.8 multiply_reduce_fusion
  105.8 2.6 multiply_convert_fusion
  108.4 5.6 all_to_all.25
  114.0 2.1 copy.26
  116.0 63.6 %all_to_all.33 = bf16[256,4,1280]{2,0,1:T(8,128)(2,1)S(1)} all-to-all(bf16[256,4,1280]{2,0,1:T(8,128)(2,1)S(1)} %copy.26), channel_id=1, replica_groups=mesh['groups'=2,'dp'=4,'tensor'=4] {'dp'}, dimensions={1} | all-to-all | bytes 5242880 | tf_op jit(solution)/shard_map/all_to_all | solution.py:63
  179.6 4.9 convolution_convert_fusion.1
  185.3 50.0 %reduce-scatter.3.cloned.1.call-done = bf16[256,1280]{1,0:T(8,128)(2,1)} async-done(((bf16[1024,1280]{1,0:T(8,128)(2,1)}), bf16[256,1280]{1,0:T(8,128)(2,1)}) %reduce-scatter.3.cloned.1.call-update) | async-done | bytes 655376 | tf_op jit(solution)/shard_map/reduce_scatter | solution.py:64
  235.3 358.0 %all-gather.2.cloned.1.call-done = bf16[1280,8192]{1,0:T(8,128)(2,1)} async-done(((bf16[1280,2048]{1,0:T(8,128)(2,1)}), bf16[1280,8192]{1,0:T(8,128)(2,1)}) %all-gather.2.cloned.1.call-update) | async-done | bytes 20971536 | tf_op jit(solution)/shard_map/all_gather | solution.py:73
  593.3 17.4 %convolution_convert_fusion = bf16[256,8192]{1,0:T(8,128)(2,1)} fusion(bf16[1280,8192]{1,0:T(8,128)(2,1)} %all-gather.2.cloned.1.call-done, bf16[256,1280]{1,0:T(8,128)(2,1)} %reduce-scatter.3.cloned.1.call-done, f32[1280]{0:T(1024)S(1)} %copy-done.13), kind=kOutput, calls=%fused_computation.8 | convolution fusion | flops 5392760832 | bytes 25826304 | tf_op jit(solution)/shard_map/dot_general | solution.py:71
  611.4 1.2 reduce-window.6
  613.7 38.8 %scatter_fusion = s32[4,64]{1,0:T(4,128)} fusion(s32[4,64]{1,0:T(4,128)} %broadcast_in_dim.23, s32[256]{0:T(256)S(1)} %bitcast.71, s32[256]{0:T(256)S(1)} %get-tuple-element.10), kind=kCustom, calls=%fused_computation | custom fusion | bytes 5120 | tf_op jit(solution)/shard_map/scatter | solution.py:103
  652.5 3.2 all-to-all-start
  655.7 1.5 add_convert_fusion.1
  658.4 48.1 %scatter_fusion.1 = bf16[4,64,2048]{2,1,0:T(8,128)(2,1)} fusion(bf16[4,64,2048]{2,1,0:T(8,128)(2,1)} %broadcast_in_dim.28, s32[256]{0:T(256)S(1)} %bitcast.72, bf16[256,2048]{1,0:T(8,128)(2,1)S(1)} %add_convert_fusion.1), kind=kCustom, calls=%fused_computation.1 | custom fusion | bytes 3147776 | tf_op jit(solution)/shard_map/scatter | solution.py:98
  706.5 4.5 all-to-all-start.2
  712.3 24.4 %all-to-all-done.2 = bf16[4,64,2048]{2,1,0:T(8,128)(2,1)} async-done(((bf16[4,64,2048]{2,1,0:T(8,128)(2,1)}), bf16[4,64,2048]{2,1,0:T(8,128)(2,1)}, u32[]{:S(2)}, u32[]{:S(2)}) %all-to-all-start.2) | async-done | bytes 1048608 | tf_op jit(solution)/shard_map/all_to_all | solution.py:106
  736.7 5.7 scatter_fusion.2
  (64 shorter events, 7.8 us)
Async XLA Ops:
  6.5 173.1 %copy-start = (bf16[1280,1280]{1,0:T(8,128)(2,1)S(1)}, bf16[1280,1280]{1,0:T(8,128)(2,1)}, u32[]{:S(2)}) copy-start(bf16[1280,1280]{1,0:T(8,128)(2,1)} %param.23) | copy-start | bytes 9830404
  6.5 2.9 copy-start.9
  6.5 95.1 %all-reduce.2.cloned.1.call-start = ((), (), s32[]{:S(2)}) async-start(), calls=%async_computation.5 | async-start | bytes 5242880 | tf_op jit(solution)/shard_map/psum | solution.py:58
  6.5 4.8 copy-start.2
  11.4 1.7 copy-start.10
  11.4 1.7 copy-start.12
  11.4 1.7 copy-start.14
  28.1 7.6 %copy-start.11 = (bf16[320,1280]{1,0:T(8,128)(2,1)S(1)}, bf16[320,1280]{1,0:T(8,128)(2,1)}, u32[]{:S(2)}) copy-start(bf16[320,1280]{1,0:T(8,128)(2,1)} %param.20) | copy-start | bytes 2457604
  38.9 62.8 %copy-start.5 = (f32[1280]{0:T(1024)S(1)}, f32[1280]{0:T(1024)}, u32[]{:S(2)}) copy-start(f32[1280]{0:T(1024)} %param.21) | copy-start | bytes 15364
  38.9 66.6 %copy-start.7 = (f32[1280]{0:T(1024)S(1)}, f32[1280]{0:T(1024)}, u32[]{:S(2)}) copy-start(f32[1280]{0:T(1024)} %param.22) | copy-start | bytes 15364
  38.9 196.4 %reduce-scatter.3.cloned.1.call-start = ((), (), s32[]{:S(2)}) async-start(), calls=%async_computation.6 | async-start | bytes 3276800 | tf_op jit(solution)/shard_map/reduce_scatter | solution.py:64
  101.7 3.8 copy-start.3
  101.7 4.1 copy-start.4
  184.5 408.8 %copy-start.13 = (f32[1280]{0:T(1024)S(1)}, f32[1280]{0:T(1024)}, u32[]{:S(2)}) copy-start(f32[1280]{0:T(1024)} %param.24) | copy-start | bytes 15364
  184.5 408.8 %all-gather.2.cloned.1.call-start = ((), (), s32[]{:S(2)}) async-start(), calls=%async_computation.7 | async-start | bytes 26214400 | tf_op jit(solution)/shard_map/all_gather | solution.py:73
  185.2 470.5 %reduce-scatter.5.cloned.1.call-start = ((), (), s32[]{:S(2)}) async-start(), calls=%async_computation.8 | async-start | bytes 5242880 | tf_op jit(solution)/shard_map/reduce_scatter | solution.py:76
  610.7 0.7 copy-start.6
  610.7 45.0 %copy-start.8 = (f32[2048]{0:T(1024)S(1)}, f32[2048]{0:T(1024)}, u32[]{:S(2)}) copy-start(f32[2048]{0:T(1024)} %param.26) | copy-start | bytes 24580
  652.5 54.0 %all-to-all-start = ((s32[4,1,64]{2,1,0:T(1,128)}), s32[4,1,64]{2,1,0:T(1,128)S(1)}, u32[]{:S(2)}, u32[]{:S(2)}) async-start(s32[4,1,64]{2,1,0:T(1,128)} %bitcast.12), calls=%async_computation | async-start | bytes 4096 | tf_op jit(solution)/shard_map/all_to_all | solution.py:107
  706.5 30.2 %all-to-all-start.2 = ((bf16[4,64,2048]{2,1,0:T(8,128)(2,1)}), bf16[4,64,2048]{2,1,0:T(8,128)(2,1)}, u32[]{:S(2)}, u32[]{:S(2)}) async-start(bf16[4,64,2048]{2,1,0:T(8,128)(2,1)} %scatter_fusion.1), calls=%async_computation.4 | async-start | bytes 2097152 | tf_op jit(solution)/shard_map/all_to_all | solution.py:106
  736.7 5.7 copy-start.1
Sparse Core Ops, SparseCore 0:
  39.0 62.6 all-reduce.1
  184.6 50.6 reduce-scatter.2
  236.9 356.3 all-gather.1
  610.8 42.9 reduce-scatter.4
where the time goes:
time: 752 us; the launch traced here: 749 us
  waiting for transfers between devices  496 us (66%)
  local copies, waits for them, and re-layouts  110 us (15%)
  blocking collectives  63.6 us (8%)
  matrix products  46.7 us (6%)
  between operations  14.6 us (2%)
  other arithmetic  10.6 us (1%)
  starting transfers between devices  8.01 us (1%)
    all_gather x1, waiting for transfers between devices, local(): lax.all_gather(w_second, 'dp', axis=1, tiled=True)  358 us
    all_to_all x1, blocking collectives, local(): lax.all_to_all(merged_in, 'dp', split_axis=1, concat_axis=0, tiled=True)  63.6 us
    psum x1, waiting for transfers between devices, local(): summed = lax.psum(partial_value, 'tensor').astype(jnp.float32)  62.5 us
    reduce_scatter x1, waiting for transfers between devices, local(): lax.psum_scatter(jnp.dot(received, w_first, preferred_element_type=jnp.fl...  50 us
    scatter x1, local copies, waits for them, and re-layouts, local(): buffer = jnp.zeros((dp_count, capacity, feature_count), jnp.bfloat16).at[...  48.1 us
    scatter x1, local copies, waits for them, and re-layouts, local(): positions = jnp.full((dp_count, capacity), seq_rows, jnp.int32).at[shard_...  38.8 us
    all_to_all x1, waiting for transfers between devices, local(): lax.all_to_all(buffer, 'dp', split_axis=0, concat_axis=0, tiled=True)  24.4 us
    dot_general x1, matrix products, local(): jnp.dot(hidden, lax.all_gather(w_second, 'dp', axis=1, tiled=True), prefe...  17.4 us
  transfers between devices with their start and end apart: 6, of which 4 were waited for; matrix products, arithmetic and copies ran while one was open for 12% of the time, Pallas kernels for 0%

commit v1 on v0

v1 whole, which is shorter than its diff:
```python
import math

import jax
import jax.numpy as jnp
from jax import lax
from jax.sharding import PartitionSpec as P

HEAD_DIM = 80
PATCHES = 1024
MERGED = 256


def rms_scale(values, gain):
    return values * lax.rsqrt(jnp.mean(values * values, axis=-1, keepdims=True) + 1e-06) * gain


def placement(dest, live_count, dp_count, seq_rows, capacity):
    merged_dev = dest.size
    live_rows = (jnp.arange(MERGED, dtype=jnp.int32)[None, :] < (live_count // 4)[:, None]).reshape(merged_dev)
    dest_flat = dest.reshape(merged_dev)
    shard_id = jnp.where(live_rows, dest_flat // seq_rows, dp_count)
    local_row = dest_flat % seq_rows
    index = jnp.arange(merged_dev, dtype=jnp.int32)
    earlier = (shard_id[:, None] == shard_id[None, :]) & (index[None, :] < index[:, None])
    rank = jnp.sum(earlier.astype(jnp.int32), axis=1)
    slot = jnp.where(live_rows & (rank < capacity), shard_id * capacity + rank, -1)
    hit = jnp.arange(dp_count * capacity, dtype=jnp.int32)[:, None] == slot[None, :]
    rows = jnp.max(jnp.where(hit, local_row[None, :], -1), axis=1)
    return hit.astype(jnp.bfloat16), rows


def attention(patches, live_count, norm_gain, qkv_weight, qkv_bias, images_dev, heads_dev):
    normed = rms_scale(patches.astype(jnp.float32), norm_gain).astype(jnp.bfloat16)
    projected = (
        jnp.einsum("rv,jvc->jrc", normed, qkv_weight, preferred_element_type=jnp.float32)
        + qkv_bias[:, None, :]
    )
    projected = projected.astype(jnp.bfloat16).reshape(3, images_dev, PATCHES, heads_dev, HEAD_DIM)
    scores = jnp.einsum(
        "iqhd,ikhd->ihqk", projected[0], projected[1], preferred_element_type=jnp.float32
    ) / math.sqrt(HEAD_DIM)
    live_keys = jnp.arange(PATCHES, dtype=jnp.int32)[None, :] < live_count[:, None]
    scores = jnp.where(live_keys[:, None, None, :], scores, jnp.float32(-1e30))
    peak_score = jnp.max(scores, axis=-1, keepdims=True)
    exponent = jnp.exp(scores - peak_score)
    weights = (exponent / jnp.sum(exponent, axis=-1, keepdims=True)).astype(jnp.bfloat16)
    attended = jnp.einsum(
        "ihqk,ikhd->iqhd", weights, projected[2], preferred_element_type=jnp.float32
    )
    return attended.astype(jnp.bfloat16).reshape(patches.shape[0], heads_dev * HEAD_DIM)


def local(
    patches,
    grids,
    dest,
    norm_gain,
    qkv_weight,
    qkv_bias,
    proj_weight,
    proj_bias,
    merge_gain,
    w_first,
    b_first,
    w_second,
    b_second,
    text_embed,
):
    rows_dev, width = patches.shape
    images_dev = grids.shape[0]
    heads_dev = qkv_weight.shape[2] // HEAD_DIM
    dp_count = lax.axis_size("dp")
    tensor_count = lax.axis_size("tensor")
    seq_rows = text_embed.shape[0]
    capacity = images_dev * (MERGED // dp_count)
    live_count = grids[:, 0] * grids[:, 1]
    permute, slot_rows = placement(dest, live_count, dp_count, seq_rows, capacity)
    arrived_rows = lax.all_to_all(
        slot_rows.reshape(dp_count, capacity), "dp", split_axis=0, concat_axis=0, tiled=True
    ).reshape(-1)

    attended = attention(patches, live_count, norm_gain, qkv_weight, qkv_bias, images_dev, heads_dev)
    partial_value = jnp.dot(attended, proj_weight, preferred_element_type=jnp.float32).astype(jnp.bfloat16)
    summed = lax.psum_scatter(partial_value, "tensor", scatter_dimension=0, tiled=True).astype(jnp.float32)
    part = rows_dev // tensor_count
    own = lax.dynamic_slice_in_dim(patches, lax.axis_index("tensor") * part, part, 0)
    resid = own.astype(jnp.float32) + summed + proj_bias
    merged_in = rms_scale(resid, merge_gain).astype(jnp.bfloat16).reshape(part // 4, 4 * width)
    sliced = lax.all_to_all(
        merged_in.reshape(part // 4, dp_count, 4 * width // dp_count), "dp", split_axis=1, concat_axis=0, tiled=False
    )
    received = lax.all_gather(sliced, "tensor", axis=1, tiled=False)
    received = received.reshape(-1, 4 * width // dp_count)
    first_out = lax.psum_scatter(
        jnp.dot(received, w_first, preferred_element_type=jnp.float32).astype(jnp.bfloat16),
        "dp",
        scatter_dimension=0,
        tiled=True,
    ).astype(jnp.float32)
    hidden = jax.nn.gelu(first_out + b_first, approximate=False).astype(jnp.bfloat16)
    hidden = jnp.dot(permute, hidden, preferred_element_type=jnp.float32).astype(jnp.bfloat16)
    slots = lax.all_gather(hidden, "dp", axis=0, tiled=True)
    second = jnp.dot(slots, w_second, preferred_element_type=jnp.float32).astype(jnp.bfloat16)
    second = lax.psum_scatter(second, "tensor", scatter_dimension=1, tiled=True)
    columns = second.shape[1]
    second = second.reshape(dp_count, dp_count, capacity, columns)
    second = lax.all_to_all(second, "dp", split_axis=1, concat_axis=0, tiled=False)
    blocks = dp_count // tensor_count
    second = second.reshape(tensor_count, blocks, dp_count * capacity, columns)
    second = lax.all_to_all(second, "tensor", split_axis=0, concat_axis=0, tiled=True)
    visual = second.transpose(2, 1, 0, 3).reshape(dp_count * capacity, -1)
    visual = (visual.astype(jnp.float32) + b_second).astype(jnp.bfloat16)
    hit = jnp.arange(seq_rows, dtype=jnp.int32)[:, None] == arrived_rows[None, :]
    placed = jnp.dot(hit.astype(jnp.bfloat16), visual, preferred_element_type=jnp.float32).astype(jnp.bfloat16)
    return jnp.where(jnp.any(hit, axis=1)[:, None], placed, text_embed)


def solution(mesh):
    in_specs = (
        P(("groups", "dp"), None),
        P(("groups", "dp"), None),
        P(("groups", "dp"), None),
        P(),
        P(None, None, "tensor"),
        P(None, "tensor"),
        P("tensor", None),
        P(),
        P(),
        P("dp", "tensor"),
        P("tensor"),
        P("tensor", "dp"),
        P("tensor"),
        P(("groups", "dp"), "tensor"),
    )
    out_specs = P(("groups", "dp"), "tensor")
    return jax.shard_map(local, mesh=mesh, in_specs=in_specs, out_specs=out_specs, check_vma=False)
```

time: 752 us -> 365 us (0.49)
  waiting for transfers between devices: 496 us -> 219 us
  local copies, waits for them, and re-layouts: 110 us -> 12.1 us
  blocking collectives: 63.6 us -> 51.9 us
    all_gather x1 -> x2, waiting for transfers between devices: 358 us -> 78 us  [the longest x1 54.4 us: local(): slots = lax.all_gather(hidden, 'dp', axis=0, tiled=True)]
    scatter x3 -> x0, local copies, waits for them, and re-layouts: 92.6 us -> none  [the longest x1 48.1 us: local(): buffer = jnp.zeros((dp_count, capacity, feature_count), jnp.bfloat16).at[...]
    reduce_scatter x1 -> x2, waiting for transfers between devices: 0.02 us -> 76.6 us  [the longest x1 39.3 us: local(): second = lax.psum_scatter(second, 'tensor', scatter_dimension=1, tiled=True)]
    psum x1 -> x0, waiting for transfers between devices: 62.5 us -> none  [local(): summed = lax.psum(partial_value, 'tensor').astype(jnp.float32)]
    all_to_all x1 -> x2, blocking collectives: 63.6 us -> 51.9 us  [the longest x1 30.3 us: local(): lax.all_to_all(second, 'dp', split_axis=1, concat_axis=0, tiled=False)]
    all_to_all x2, waiting for transfers between devices: 24.4 us -> 13.1 us  [the longest x1 13.1 us: local(): lax.all_to_all(second, 'tensor', split_axis=0, concat_axis=0, tiled=True)]
    dot_general x3 -> x5, matrix products: 27.9 us -> 28.9 us  [the longest x1 9.96 us: local(): jnp.dot(slots, w_second, preferred_element_type=jnp.float32)]
  transfers between devices with their start and end apart: 6 -> 7, of which waited for: 4 -> 6; matrix products, arithmetic and copies ran while one was open for 12% -> 1% of each run, Pallas kernels for 0% -> 0%
where the time goes in v1:
time: 365 us
  waiting for transfers between devices  219 us (60%)
  blocking collectives  51.9 us (14%)
  matrix products  49.7 us (14%)
  between operations  14.6 us (4%)
  local copies, waits for them, and re-layouts  12.1 us (3%)
  other arithmetic  9.24 us (3%)
  starting transfers between devices  7.77 us (2%)
    all_gather x1, waiting for transfers between devices, local(): slots = lax.all_gather(hidden, 'dp', axis=0, tiled=True)  54.4 us
    reduce_scatter x1, waiting for transfers between devices, local(): lax.psum_scatter(jnp.dot(received, w_first, preferred_element_type=jnp.fl...  51.5 us
    reduce_scatter x1, waiting for transfers between devices, local(): second = lax.psum_scatter(second, 'tensor', scatter_dimension=1, tiled=True)  39.3 us
    reduce_scatter x1, waiting for transfers between devices, local(): lax.psum_scatter(partial_value, 'tensor', scatter_dimension=0, tiled=True)  37.3 us
    all_to_all x1, blocking collectives, local(): lax.all_to_all(second, 'dp', split_axis=1, concat_axis=0, tiled=False)  30.3 us
    all_gather x1, waiting for transfers between devices, local(): received = lax.all_gather(sliced, 'tensor', axis=1, tiled=False)  23.6 us
    all_to_all x1, blocking collectives, local(): lax.all_to_all(merged_in.reshape(part // 4, dp_count, 4 * width // dp_cou...  21.7 us
    all_to_all x1, waiting for transfers between devices, local(): lax.all_to_all(second, 'tensor', split_axis=0, concat_axis=0, tiled=True)  13.1 us
  transfers between devices with their start and end apart: 7, of which 6 were waited for; matrix products, arithmetic and copies ran while one was open for 1% of the time, Pallas kernels for 0%

profile of v1, /device:TPU:0, one launch (start us, length us, event | category | flops | bytes accessed | tf_op | source)
XLA Modules:
  0.0 364.5 jit_solution(5722209343498737713)
XLA Ops:
  6.5 2.5 fusion.6
  9.2 4.5 %fusion.16 = bf16[3,1024,320]{1,2,0:T(8,128)(2,1)S(1)} fusion(f32[3,320]{1,0:T(4,128)} %param.19, bf16[3,1280,320]{1,2,0:T(8,128)(2,1)} %param.18, bf16[1024,1280]{1,0:T(8,128)(2,1)S(1)} %copy-done.1, f32[1280]{0:T(1024)S(1)} %copy-done.10, f32[1024]{0:T(1024)S(1)} %add_rsqrt_fusion), kind=kOutput, calls=%fused_computation.27 | convolution fusion | flops 2523791360 | bytes 7058176 | tf_op jit(solution)/shard_map/rv,jvc->jrc/dot_general | solution.py:35
  17.0 10.9 %fusion.106 = (f32[4,1024]{1,0:T(4,128)S(1)}, f32[4,1024,1024]{1,2,0:T(8,128)}) fusion(pred[1024]{0:T(1024)(128)(4,1)S(1)} %iota_compare_fusion.5, bf16[1024,4,80]{0,2,1:T(8,128)(2,1)} %bitcast.59, bf16[1024,4,80]{0,2,1:T(8,128)(2,1)} %bitcast.58), kind=kOutput, calls=%fused_computation.141 | convolution fusion | flops 687866880 | bytes 18105344 | tf_op jit(solution)/shard_map/sub | solution.py:45
  27.9 7.6 %fusion.21 = bf16[4,80,1024]{2,1,0:T(8,128)(2,1)S(1)} fusion(bf16[1024,4,80]{0,2,1:T(8,128)(2,1)} %bitcast.57, f32[4,1024,1024]{1,2,0:T(8,128)} %get-tuple-element.14, f32[4,1024]{1,0:T(4,128)S(1)} %get-tuple-element.13), kind=kOutput, calls=%fused_computation.30 | convolution fusion | flops 679804928 | bytes 18104320 | tf_op jit(solution)/shard_map/ihqk,ikhd->iqhd/dot_general | solution.py:47
  35.5 3.1 convolution_convert_fusion.2
  38.7 37.3 %reduce-scatter.4.cloned.1.call-done = bf16[256,1280]{1,0:T(8,128)(2,1)} async-done(((bf16[1024,1280]{1,0:T(8,128)(2,1)}), bf16[256,1280]{1,0:T(8,128)(2,1)}) %reduce-scatter.4.cloned.1.call-update) | async-done | bytes 655376 | tf_op jit(solution)/shard_map/reduce_scatter | solution.py:84
  76.0 1.7 multiply_reduce_fusion
  77.7 2.2 multiply_convert_fusion
  79.9 2.3 broadcast_in_dim_reshape_reshape.3
  83.4 21.7 %all_to_all.44 = bf16[1,64,4,1280]{3,1,0,2:T(8,128)(2,1)} all-to-all(bf16[1,64,4,1280]{3,1,0,2:T(8,128)(2,1)S(1)} %copy.26), channel_id=1, replica_groups=mesh['groups'=2,'dp'=4,'tensor'=4] {'dp'}, dimensions={2} | all-to-all | bytes 1310720 | tf_op jit(solution)/shard_map/all_to_all | solution.py:89
  105.3 23.6 %all-gather.6.cloned.1.call-done = bf16[4,4,64,1,1280]{4,2,1,0,3:T(8,128)(2,1)} async-done(((bf16[4,1,64,1,1280]{4,2,1,0,3:T(8,128)(2,1)}), bf16[4,4,64,1,1280]{4,2,1,0,3:T(8,128)(2,1)}) %all-gather.6.cloned.1.call-update) | async-done | bytes 2621456 | tf_op jit(solution)/shard_map/all_gather | solution.py:92
  128.9 6.8 %convolution_convert_fusion.1 = bf16[1024,1280]{1,0:T(8,128)(2,1)} fusion(bf16[1024,1280]{1,0:T(8,128)(2,1)} %bitcast.66, bf16[1280,1280]{1,0:T(8,128)(2,1)S(1)} %copy-done), kind=kOutput, calls=%fused_computation.16 | convolution fusion | flops 3356753920 | bytes 8519680 | tf_op jit(solution)/shard_map/dot_general | solution.py:95
  136.6 51.5 %reduce-scatter.6.cloned.1.call-done = bf16[256,1280]{1,0:T(8,128)(2,1)} async-done(((bf16[1024,1280]{1,0:T(8,128)(2,1)}), bf16[256,1280]{1,0:T(8,128)(2,1)}) %reduce-scatter.6.cloned.1.call-update) | async-done | bytes 655376 | tf_op jit(solution)/shard_map/reduce_scatter | solution.py:94
  188.1 5.1 %convolution_convert_fusion.4 = bf16[256,1280]{1,0:T(8,128)(2,1)} fusion(bf16[256,1280]{1,0:T(8,128)(2,1)} %reduce-scatter.6.cloned.1.call-done, f32[1280]{0:T(1024)S(1)} %copy-done.11, s32[256]{0:T(256)S(1)} %bitcast.61), kind=kOutput, calls=%fused_computation.24 | convolution fusion | flops 190119936 | bytes 1316864 | tf_op jit(solution)/shard_map/dot_general | solution.py:101
  193.2 54.4 %all-gather.4.cloned.1.call-done = bf16[1024,1280]{1,0:T(8,128)(2,1)} async-done(((bf16[256,1280]{1,0:T(8,128)(2,1)}), bf16[1024,1280]{1,0:T(8,128)(2,1)}) %all-gather.4.cloned.1.call-update) | async-done | bytes 2621456 | tf_op jit(solution)/shard_map/all_gather | solution.py:102
  247.7 10.0 %convolution_convert_fusion = bf16[1024,2048]{1,0:T(8,128)(2,1)} fusion(bf16[1024,1280]{1,0:T(8,128)(2,1)} %all-gather.4.cloned.1.call-done, bf16[1280,2048]{1,0:T(8,128)(2,1)} %param.25), kind=kOutput, calls=%fused_computation.15 | convolution fusion | flops 5370806272 | bytes 12058624 | tf_op jit(solution)/shard_map/dot_general | solution.py:103
  258.4 3.2 all-to-all-start
  261.6 39.3 %reduce-scatter.8.cloned.1.call-done = bf16[1024,512]{1,0:T(8,128)(2,1)} async-done(((bf16[1024,2048]{1,0:T(8,128)(2,1)}), bf16[1024,512]{1,0:T(8,128)(2,1)}) %reduce-scatter.8.cloned.1.call-update) | async-done | bytes 1048592 | tf_op jit(solution)/shard_map/reduce_scatter | solution.py:104
  301.0 2.3 copy.27
  303.3 30.3 %all_to_all.45 = bf16[1,4,4,64,512]{4,3,1,0,2:T(8,128)(2,1)} all-to-all(bf16[1,4,4,64,512]{4,3,1,0,2:T(8,128)(2,1)} %copy.27), channel_id=1, replica_groups=mesh['groups'=2,'dp'=4,'tensor'=4] {'dp'}, dimensions={2} | all-to-all | bytes 2097152 | tf_op jit(solution)/shard_map/all_to_all | solution.py:107
  333.5 4.2 %all-to-all-start.3 = ((bf16[4,1,256,512]{3,2,1,0:T(8,128)(2,1)}), bf16[4,1,256,512]{3,2,1,0:T(8,128)(2,1)}, u32[]{:S(2)}, u32[]{:S(2)}) async-start(bf16[4,1,256,512]{3,2,1,0:T(8,128)(2,1)} %bitcast.54), calls=%async_computation.6 | async-start | bytes 2097152 | tf_op jit(solution)/shard_map/all_to_all | solution.py:110
  339.2 13.1 %all-to-all-done.3 = bf16[4,1,256,512]{3,2,1,0:T(8,128)(2,1)} async-done(((bf16[4,1,256,512]{3,2,1,0:T(8,128)(2,1)}), bf16[4,1,256,512]{3,2,1,0:T(8,128)(2,1)}, u32[]{:S(2)}, u32[]{:S(2)}) %all-to-all-start.3) | async-done | bytes 1048608 | tf_op jit(solution)/shard_map/all_to_all | solution.py:110
  352.3 2.3 copy.29
  356.2 1.8 fusion.14
  (53 shorter events, 8.6 us)
Async XLA Ops:
  6.5 122.3 %copy-start = (bf16[1280,1280]{1,0:T(8,128)(2,1)S(1)}, bf16[1280,1280]{1,0:T(8,128)(2,1)}, u32[]{:S(2)}) copy-start(bf16[1280,1280]{1,0:T(8,128)(2,1)} %param.23) | copy-start | bytes 9830404
  6.5 2.5 copy-start.10
  6.5 69.5 %reduce-scatter.4.cloned.1.call-start = ((), (), s32[]{:S(2)}) async-start(), calls=%async_computation.7 | async-start | bytes 3276800 | tf_op jit(solution)/shard_map/reduce_scatter | solution.py:84
  6.5 2.7 copy-start.1
  13.7 1.3 copy-start.7
  27.9 7.6 %copy-start.9 = (bf16[320,1280]{1,0:T(8,128)(2,1)S(1)}, bf16[320,1280]{1,0:T(8,128)(2,1)}, u32[]{:S(2)}) copy-start(bf16[320,1280]{1,0:T(8,128)(2,1)} %param.20) | copy-start | bytes 2457604
  38.6 37.4 %copy-start.4 = (f32[1280]{0:T(1024)S(1)}, f32[1280]{0:T(1024)}, u32[]{:S(2)}) copy-start(f32[1280]{0:T(1024)} %param.21) | copy-start | bytes 15364
  38.6 39.1 %copy-start.5 = (f32[1280]{0:T(1024)S(1)}, f32[1280]{0:T(1024)}, u32[]{:S(2)}) copy-start(f32[1280]{0:T(1024)} %param.22) | copy-start | bytes 15364
  38.7 90.2 %all-gather.6.cloned.1.call-start = ((), (), s32[]{:S(2)}) async-start(), calls=%async_computation.11 | async-start | bytes 3276800 | tf_op jit(solution)/shard_map/all_gather | solution.py:92
  76.0 1.7 copy-start.2
  105.1 83.0 %reduce-scatter.6.cloned.1.call-start = ((), (), s32[]{:S(2)}) async-start(), calls=%async_computation.8 | async-start | bytes 3276800 | tf_op jit(solution)/shard_map/reduce_scatter | solution.py:94
  135.7 0.7 copy-start.8
  135.7 52.4 %copy-start.11 = (f32[1280]{0:T(1024)S(1)}, f32[1280]{0:T(1024)}, u32[]{:S(2)}) copy-start(f32[1280]{0:T(1024)} %param.24) | copy-start | bytes 15364
  135.7 112.0 %all-gather.4.cloned.1.call-start = ((), (), s32[]{:S(2)}) async-start(), calls=%async_computation.9 | async-start | bytes 3276800 | tf_op jit(solution)/shard_map/all_gather | solution.py:102
  193.2 107.8 %reduce-scatter.8.cloned.1.call-start = ((), (), s32[]{:S(2)}) async-start(), calls=%async_computation.10 | async-start | bytes 5242880 | tf_op jit(solution)/shard_map/reduce_scatter | solution.py:104
  258.4 44.8 %all-to-all-start = ((s32[4,1,64]{2,1,0:T(1,128)}), s32[4,1,64]{2,1,0:T(1,128)S(1)}, u32[]{:S(2)}, u32[]{:S(2)}) async-start(s32[4,1,64]{2,1,0:T(1,128)} %all_to_all.31), calls=%async_computation | async-start | bytes 4096 | tf_op jit(solution)/shard_map/all_to_all | solution.py:78
  333.5 18.7 %all-to-all-start.3 = ((bf16[4,1,256,512]{3,2,1,0:T(8,128)(2,1)}), bf16[4,1,256,512]{3,2,1,0:T(8,128)(2,1)}, u32[]{:S(2)}, u32[]{:S(2)}) async-start(bf16[4,1,256,512]{3,2,1,0:T(8,128)(2,1)} %bitcast.54), calls=%async_computation.6 | async-start | bytes 2097152 | tf_op jit(solution)/shard_map/all_to_all | solution.py:110
  337.8 16.8 %copy-start.6 = (f32[2048]{0:T(1024)S(1)}, f32[2048]{0:T(1024)}, u32[]{:S(2)}) copy-start(f32[2048]{0:T(1024)} %param.26) | copy-start | bytes 24580
  354.5 1.7 copy-start.3
Sparse Core Ops, SparseCore 0:
  38.8 37.1 reduce-scatter.3
  105.2 23.6 all-gather.5
  135.8 52.2 reduce-scatter.5
  193.3 54.2 all-gather.3
  257.8 43.1 reduce-scatter.7

commit v2 on v1

--- a/solution.py
+++ b/solution.py
@@ -1,9 +1,14 @@
+import functools
 import math
 
 import jax
 import jax.numpy as jnp
 from jax import lax
+from jax.experimental import pallas as pl
+from jax.experimental.pallas import tpu as pltpu
 from jax.sharding import PartitionSpec as P
+
+MESH = pl.DeviceIdType.MESH
 
 HEAD_DIM = 80
 PATCHES = 1024
@@ -48,6 +53,280 @@
         "ihqk,ikhd->iqhd", weights, projected[2], preferred_element_type=jnp.float32
     )
     return attended.astype(jnp.bfloat16).reshape(patches.shape[0], heads_dev * HEAD_DIM)
+
+
+def merger_kernel(
+    n, x_hbm, w1_hbm, bias, permute, w2_hbm, out_hbm,
+    x, w1, w2, part, from_left, from_right, total, slots, acc, out,
+    load_sem, sum_send, sum_recv, hid_send, hid_recv,
+):
+    chunks, _, block, wide = part.shape
+    me = lax.axis_index("dp")
+    left, right = lax.max(me - 1, 0), lax.min(me + 1, n - 1)
+    has_left, has_right = me > 0, me < n - 1
+    inner = has_left & has_right
+
+    loads = [
+        pltpu.make_async_copy(a, b, load_sem.at[i])
+        for i, (a, b) in enumerate(((x_hbm, x), (w1_hbm, w1), (w2_hbm, w2)))
+    ]
+    for load in loads:
+        load.start()
+
+    barrier = pltpu.get_barrier_semaphore()
+
+    @pl.when(has_left)
+    def _():
+        pl.semaphore_signal(barrier, inc=1, device_id={"dp": left}, device_id_type=MESH)
+
+    @pl.when(has_right)
+    def _():
+        pl.semaphore_signal(barrier, inc=1, device_id={"dp": right}, device_id_type=MESH)
+
+    pl.semaphore_wait(barrier, has_left.astype(jnp.int32) + has_right.astype(jnp.int32))
+
+    def sum_right(c, b):
+        return pltpu.make_async_remote_copy(
+            part.at[c, b], from_left.at[c, b], sum_send.at[0, c, b], sum_recv.at[0, c, b],
+            device_id={"dp": right}, device_id_type=MESH)
+
+    def sum_left(c, b):
+        return pltpu.make_async_remote_copy(
+            part.at[c, b], from_right.at[c, b], sum_send.at[1, c, b], sum_recv.at[1, c, b],
+            device_id={"dp": left}, device_id_type=MESH)
+
+    def hid_right(c, b):
+        return pltpu.make_async_remote_copy(
+            slots.at[c, b], slots.at[c, b], hid_send.at[0, c, b], hid_recv.at[0, c, b],
+            device_id={"dp": right}, device_id_type=MESH)
+
+    def hid_left(c, b):
+        return pltpu.make_async_remote_copy(
+            slots.at[c, b], slots.at[c, b], hid_send.at[1, c, b], hid_recv.at[1, c, b],
+            device_id={"dp": left}, device_id_type=MESH)
+
+    def first(c):
+        columns = pl.ds(pl.multiple_of(c * wide, wide), wide)
+
+        def tile(b):
+            part[c, b] = jnp.dot(
+                x[pl.ds(pl.multiple_of(b * block, block), block), :], w1[:, columns],
+                preferred_element_type=jnp.float32,
+            ).astype(jnp.bfloat16)
+
+        def up(i, carry):
+            b = n - 1 - i
+            tile(b)
+
+            @pl.when((me == 0) & (b > 0))
+            def _():
+                sum_right(c, b).start()
+
+            return carry
+
+        def down(b, carry):
+            tile(b)
+
+            @pl.when((me == n - 1) & (b < n - 1))
+            def _():
+                sum_left(c, b).start()
+
+            return carry
+
+        @pl.when(me == 0)
+        def _():
+            lax.fori_loop(0, n, up, 0)
+
+        @pl.when(me > 0)
+        def _():
+            lax.fori_loop(0, n, down, 0)
+
+    def relay(c):
+        def one(i, carry):
+            b = n - 1 - i
+
+            @pl.when(inner & (b > me))
+            def _():
+                sum_right(c, b).wait_recv()
+                part[c, b] = (part[c, b].astype(jnp.float32) + from_left[c, b].astype(jnp.float32)).astype(jnp.bfloat16)
+                sum_right(c, b).start()
+
+            @pl.when(inner & (i < me))
+            def _():
+                sum_left(c, i).wait_recv()
+                part[c, i] = (part[c, i].astype(jnp.float32) + from_right[c, i].astype(jnp.float32)).astype(jnp.bfloat16)
+                sum_left(c, i).start()
+
+            return carry
+
+        lax.fori_loop(0, n, one, 0)
+
+    def activate(c):
+        total[...] = part[c, me].astype(jnp.float32) + bias[c]
+
+        @pl.when(has_left)
+        def _():
+            sum_right(c, me).wait_recv()
+            total[...] += from_left[c, me].astype(jnp.float32)
+
+        @pl.when(has_right)
+        def _():
+            sum_left(c, me).wait_recv()
+            total[...] += from_right[c, me].astype(jnp.float32)
+
+        value = total[...]
+        hidden = (0.5 * value * (1.0 + lax.erf(value * math.sqrt(0.5)))).astype(jnp.bfloat16)
+        slots[c, me] = jnp.dot(permute[...], hidden, preferred_element_type=jnp.float32).astype(jnp.bfloat16)
+
+        @pl.when(has_right)
+        def _():
+            hid_right(c, me).start()
+
+        @pl.when(has_left)
+        def _():
+            hid_left(c, me).start()
+
+    def spread(c):
+        def one(k, carry):
+            before, after = me - k, me + k
+
+            @pl.when(before >= 0)
+            def _():
+                hid_right(c, before).wait_recv()
+
+                @pl.when(has_right)
+                def _():
+                    hid_right(c, before).start()
+
+            @pl.when(after < n)
+            def _():
+                hid_left(c, after).wait_recv()
+
+                @pl.when(has_left)
+                def _():
+                    hid_left(c, after).start()
+
+            return carry
+
+        lax.fori_loop(1, n, one, 0)
+
+    def second(c):
+        depth = pl.ds(pl.multiple_of(c * wide, wide), wide)
+
+        def one(b, carry):
+            rows = pl.ds(pl.multiple_of(b * block, block), block)
+            more = jnp.dot(slots[c, b], w2[depth, :], preferred_element_type=jnp.float32)
+
+            @pl.when(c == 0)
+            def _():
+                acc[rows, :] = more
+
+            @pl.when(c > 0)
+            def _():
+                acc[rows, :] += more
+
+            return carry
+
+        lax.fori_loop(0, n, one, 0)
+
+    loads[0].wait()
+    loads[1].wait()
+    first(0)
+    loads[2].wait()
+
+    def step(s, carry):
+        @pl.when(s + 1 < chunks)
+        def _():
+            first(s + 1)
+
+        @pl.when(s < chunks)
+        def _():
+            relay(s)
+
+        @pl.when((s >= 1) & (s <= chunks))
+        def _():
+            activate(s - 1)
+
+        @pl.when(s >= 2)
+        def _():
+            spread(s - 2)
+            second(s - 2)
+
+        return carry
+
+    lax.fori_loop(0, chunks + 2, step, 0)
+
+    def finish(b, carry):
+        rows = pl.ds(pl.multiple_of(b * block, block), block)
+        out[rows, :] = acc[rows, :].astype(jnp.bfloat16)
+        return carry
+
+    lax.fori_loop(0, n, finish, 0)
+    store = pltpu.make_async_copy(out, out_hbm, load_sem.at[0])
+    store.start()
+
+    def drain(c, carry):
+        def one(b, inside):
+            @pl.when(has_right & (b > me))
+            def _():
+                sum_right(c, b).wait_send()
+
+            @pl.when(has_left & (b < me))
+            def _():
+                sum_left(c, b).wait_send()
+
+            @pl.when(has_right & (b <= me))
+            def _():
+                hid_right(c, b).wait_send()
+
+            @pl.when(has_left & (b >= me))
+            def _():
+                hid_left(c, b).wait_send()
+
+            return inside
+
+        return lax.fori_loop(0, n, one, carry)
+
+    lax.fori_loop(0, chunks, drain, 0)
+    store.wait()
+
+
+def merger(x, w1, bias, permute, w2):
+    n = lax.axis_size("dp")
+    rows, depth = x.shape
+    hidden, columns = w2.shape
+    block = rows // n
+    wide = 256 if hidden % 256 == 0 else 128
+    chunks = hidden // wide
+    any_space = pl.BlockSpec(memory_space=pl.ANY)
+    vmem = pl.BlockSpec(memory_space=pltpu.VMEM)
+    stack = pltpu.VMEM((chunks, n, block, wide), jnp.bfloat16)
+    return pl.pallas_call(
+        functools.partial(merger_kernel, n),
+        out_shape=jax.ShapeDtypeStruct((rows, columns), jnp.bfloat16),
+        in_specs=[any_space, any_space, vmem, vmem, any_space],
+        out_specs=any_space,
+        scratch_shapes=[
+            pltpu.VMEM((rows, depth), jnp.bfloat16),
+            pltpu.VMEM((depth, hidden), jnp.bfloat16),
+            pltpu.VMEM((hidden, columns), jnp.bfloat16),
+            stack,
+            stack,
+            stack,
+            pltpu.VMEM((block, wide), jnp.float32),
+            stack,
+            pltpu.VMEM((rows, columns), jnp.float32),
+            pltpu.VMEM((rows, columns), jnp.bfloat16),
+            pltpu.SemaphoreType.DMA((3,)),
+            pltpu.SemaphoreType.DMA((2, chunks, n)),
+            pltpu.SemaphoreType.DMA((2, chunks, n)),
+            pltpu.SemaphoreType.DMA((2, chunks, n)),
+            pltpu.SemaphoreType.DMA((2, chunks, n)),
+        ],
+        compiler_params=pltpu.CompilerParams(
+            collective_id=0, has_side_effects=True, vmem_limit_bytes=60 * 1024 * 1024
+        ),
+    )(x, w1, bias.reshape(chunks, 1, wide), permute, w2)
 
 
 def local(
@@ -91,16 +370,7 @@
     )
     received = lax.all_gather(sliced, "tensor", axis=1, tiled=False)
     received = received.reshape(-1, 4 * width // dp_count)
-    first_out = lax.psum_scatter(
-        jnp.dot(received, w_first, preferred_element_type=jnp.float32).astype(jnp.bfloat16),
-        "dp",
-        scatter_dimension=0,
-        tiled=True,
-    ).astype(jnp.float32)
-    hidden = jax.nn.gelu(first_out + b_first, approximate=False).astype(jnp.bfloat16)
-    hidden = jnp.dot(permute, hidden, preferred_element_type=jnp.float32).astype(jnp.bfloat16)
-    slots = lax.all_gather(hidden, "dp", axis=0, tiled=True)
-    second = jnp.dot(slots, w_second, preferred_element_type=jnp.float32).astype(jnp.bfloat16)
+    second = merger(received, w_first, b_first, permute, w_second)
     second = lax.psum_scatter(second, "tensor", scatter_dimension=1, tiled=True)
     columns = second.shape[1]
     second = second.reshape(dp_count, dp_count, capacity, columns)

time: 365 us -> 344 us (0.942)
  Pallas kernels: 0 us -> 108 us
  waiting for transfers between devices: 219 us -> 112 us
  matrix products: 49.7 us -> 28.1 us
    pallas_call x0 -> x1, Pallas kernels: none -> 108 us  [merger(): pl.pallas_call(functools.partial(merger_kernel, n), out_shape=jax.ShapeDt...]
    all_gather x1 -> x0, waiting for transfers between devices: 54.4 us -> none  [local(): slots = lax.all_gather(hidden, 'dp', axis=0, tiled=True)]
    reduce_scatter x1 -> x0, waiting for transfers between devices: 51.5 us -> none  [local(): lax.psum_scatter(jnp.dot(received, w_first, preferred_element_type=jnp.fl...]
    dot_general x3 -> x0, matrix products: 21.8 us -> none  [the longest x1 9.96 us: local(): jnp.dot(slots, w_second, preferred_element_type=jnp.float32)]
  transfers between devices with their start and end apart: 7 -> 5, of which waited for: 6 -> 4; matrix products, arithmetic and copies ran while one was open for 1% -> 1% of each run, Pallas kernels for 0% -> 0%
where the time goes in v2:
time: 344 us; the launch traced here: 343 us
  waiting for transfers between devices  112 us (33%)
  Pallas kernels  108 us (31%)
  blocking collectives  51.7 us (15%)
  matrix products  28.1 us (8%)
  between operations  14.5 us (4%)
  local copies, waits for them, and re-layouts  12.9 us (4%)
  other arithmetic  9.11 us (3%)
  starting transfers between devices  6.99 us (2%)
    pallas_call x1, Pallas kernels, merger(): pl.pallas_call(functools.partial(merger_kernel, n), out_shape=jax.ShapeDt...  108 us
    reduce_scatter x1, waiting for transfers between devices, local(): second = lax.psum_scatter(second, 'tensor', scatter_dimension=1, tiled=True)  39.2 us
    reduce_scatter x1, waiting for transfers between devices, local(): lax.psum_scatter(partial_value, 'tensor', scatter_dimension=0, tiled=True)  37.3 us
    all_to_all x1, blocking collectives, local(): lax.all_to_all(second, 'dp', split_axis=1, concat_axis=0, tiled=False)  30.1 us
    all_gather x1, waiting for transfers between devices, local(): received = lax.all_gather(sliced, 'tensor', axis=1, tiled=False)  22.2 us
    all_to_all x1, blocking collectives, local(): lax.all_to_all(merged_in.reshape(part // 4, dp_count, 4 * width // dp_cou...  21.6 us
    all_to_all x1, waiting for transfers between devices, local(): lax.all_to_all(second, 'tensor', split_axis=0, concat_axis=0, tiled=True)  13 us
    sub x1, matrix products, attention(): exponent = jnp.exp(scores - peak_score)  10.9 us
  transfers between devices with their start and end apart: 5, of which 4 were waited for; matrix products, arithmetic and copies ran while one was open for 1% of the time, Pallas kernels for 0%

profile of v2, /device:TPU:0, one launch (start us, length us, event | category | flops | bytes accessed | tf_op | source)
XLA Modules:
  0.0 343.2 jit_solution(10290207671660664707)
XLA Ops:
  6.5 2.5 fusion.6
  9.8 3.5 %fusion.16 = bf16[3,1024,320]{1,2,0:T(8,128)(2,1)S(1)} fusion(f32[3,320]{1,0:T(4,128)} %param.19, bf16[3,1280,320]{1,2,0:T(8,128)(2,1)S(1)} %copy-done, bf16[1024,1280]{1,0:T(8,128)(2,1)S(1)} %copy-done.1, f32[1280]{0:T(1024)S(1)} %copy-done.9, f32[1024]{0:T(1024)S(1)} %add_rsqrt_fusion), kind=kOutput, calls=%fused_computation.24 | convolution fusion | flops 2523791360 | bytes 7058176 | tf_op jit(solution)/shard_map/rv,jvc->jrc/dot_general | solution.py:40
  13.3 1.3 fusion.29
  16.5 10.9 %fusion.31 = (f32[4,1024]{1,0:T(4,128)S(1)}, f32[4,1024,1024]{1,2,0:T(8,128)}) fusion(pred[1024]{0:T(1024)(128)(4,1)S(1)} %iota_compare_fusion.4, bf16[1024,4,80]{0,2,1:T(8,128)(2,1)} %bitcast.58, bf16[1024,4,80]{0,2,1:T(8,128)(2,1)} %bitcast.57), kind=kOutput, calls=%fused_computation.55 | convolution fusion | flops 687866880 | bytes 18105344 | tf_op jit(solution)/shard_map/sub | solution.py:50
  27.4 7.4 %fusion.21 = bf16[4,80,1024]{2,1,0:T(8,128)(2,1)S(1)} fusion(bf16[1024,4,80]{0,2,1:T(8,128)(2,1)S(1)} %bitcast.56, f32[4,1024,1024]{1,2,0:T(8,128)} %get-tuple-element.14, f32[4,1024]{1,0:T(4,128)S(1)} %get-tuple-element.13), kind=kOutput, calls=%fused_computation.26 | convolution fusion | flops 679804928 | bytes 18104320 | tf_op jit(solution)/shard_map/ihqk,ikhd->iqhd/dot_general | solution.py:52
  34.9 3.1 convolution_convert_fusion
  38.0 37.3 %reduce-scatter.3.cloned.1.call-done = bf16[256,1280]{1,0:T(8,128)(2,1)} async-done(((bf16[1024,1280]{1,0:T(8,128)(2,1)}), bf16[256,1280]{1,0:T(8,128)(2,1)}) %reduce-scatter.3.cloned.1.call-update) | async-done | bytes 655376 | tf_op jit(solution)/shard_map/reduce_scatter | solution.py:363
  75.3 1.6 multiply_reduce_fusion
  77.0 1.6 multiply_convert_fusion
  78.6 1.0 broadcast_in_dim_reshape_reshape.3
  79.6 1.2 copy.35
  80.7 21.6 %all_to_all.44 = bf16[1,64,4,1280]{3,1,0,2:T(8,128)(2,1)} all-to-all(bf16[1,64,4,1280]{3,1,0,2:T(8,128)(2,1)S(1)} %copy.35), channel_id=1, replica_groups=mesh['groups'=2,'dp'=4,'tensor'=4] {'dp'}, dimensions={2} | all-to-all | bytes 1310720 | tf_op jit(solution)/shard_map/all_to_all | solution.py:368
  104.0 22.2 %all-gather.3.cloned.1.call-done = bf16[4,4,64,1,1280]{4,2,3,0,1:T(8,128)(2,1)} async-done(((bf16[4,1,64,1,1280]{4,2,3,0,1:T(8,128)(2,1)}), bf16[4,4,64,1,1280]{4,2,3,0,1:T(8,128)(2,1)}) %all-gather.3.cloned.1.call-update) | async-done | bytes 2621456 | tf_op jit(solution)/shard_map/all_gather | solution.py:371
  126.2 3.5 %copy.37 = bf16[4,4,64,1,1280]{4,2,1,0,3:T(8,128)(2,1)} copy(bf16[4,4,64,1,1280]{4,2,3,0,1:T(8,128)(2,1)} %all-gather.3.cloned.1.call-done) | data formatting | bytes 5242880 | tf_op jit(solution)/shard_map/all_gather | solution.py:371
  129.8 108.1 %shard_map.136 = bf16[1024,2048]{1,0:T(8,128)(2,1)} custom-call(bf16[1024,1280]{1,0:T(8,128)(2,1)} %bitcast.52, bf16[1280,1280]{1,0:T(8,128)(2,1)} %w1_hbm.1, f32[5,1,256]{2,1,0:T(1,128)} %reshape.161.bias, bf16[256,256]{1,0:T(8,128)(2,1)} %fusion.23.permute, bf16[1280,2048]{1,0:T(8,128)(2,1)} %w2_hbm.1), custom_call_target="tpu_custom_call" | custom-call | tf_op jit(solution)/shard_map/pallas_call | solution.py:304
  238.7 3.3 all-to-all-start
  241.9 39.2 %reduce-scatter.5.cloned.1.call-done = bf16[1024,512]{1,0:T(8,128)(2,1)} async-done(((bf16[1024,2048]{1,0:T(8,128)(2,1)}), bf16[1024,512]{1,0:T(8,128)(2,1)}) %reduce-scatter.5.cloned.1.call-update) | async-done | bytes 1048592 | tf_op jit(solution)/shard_map/reduce_scatter | solution.py:374
  281.2 1.3 copy.38
  282.5 30.1 %all_to_all.45 = bf16[1,4,4,64,512]{4,3,1,0,2:T(8,128)(2,1)} all-to-all(bf16[1,4,4,64,512]{4,3,1,0,2:T(8,128)(2,1)S(1)} %copy.38), channel_id=1, replica_groups=mesh['groups'=2,'dp'=4,'tensor'=4] {'dp'}, dimensions={2} | all-to-all | bytes 2097152 | tf_op jit(solution)/shard_map/all_to_all | solution.py:377
  312.6 3.6 %all-to-all-start.3 = ((bf16[4,1,256,512]{3,2,1,0:T(8,128)(2,1)}), bf16[4,1,256,512]{3,2,1,0:T(8,128)(2,1)S(1)}, u32[]{:S(2)}, u32[]{:S(2)}) async-start(bf16[4,1,256,512]{3,2,1,0:T(8,128)(2,1)} %bitcast.53), calls=%async_computation.5 | async-start | bytes 2097152 | tf_op jit(solution)/shard_map/all_to_all | solution.py:380
  317.6 13.0 %all-to-all-done.3 = bf16[4,1,256,512]{3,2,1,0:T(8,128)(2,1)S(1)} async-done(((bf16[4,1,256,512]{3,2,1,0:T(8,128)(2,1)}), bf16[4,1,256,512]{3,2,1,0:T(8,128)(2,1)S(1)}, u32[]{:S(2)}, u32[]{:S(2)}) %all-to-all-start.3) | async-done | bytes 1048608 | tf_op jit(solution)/shard_map/all_to_all | solution.py:380
  330.6 1.3 copy.40
  331.9 1.6 fusion.15
  333.5 3.2 fusion.14
  (44 shorter events, 5.4 us)
Async XLA Ops:
  6.5 2.5 copy-start
  6.5 2.5 copy-start.9
  6.5 68.8 %reduce-scatter.3.cloned.1.call-start = ((), (), s32[]{:S(2)}) async-start(), calls=%async_computation.6 | async-start | bytes 3276800 | tf_op jit(solution)/shard_map/reduce_scatter | solution.py:363
  6.5 3.3 copy-start.1
  13.3 1.3 copy-start.6
  27.4 7.4 %copy-start.8 = (bf16[320,1280]{1,0:T(8,128)(2,1)S(1)}, bf16[320,1280]{1,0:T(8,128)(2,1)}, u32[]{:S(2)}) copy-start(bf16[320,1280]{1,0:T(8,128)(2,1)} %param.20) | copy-start | bytes 2457604
  37.9 37.4 %copy-start.2 = (f32[1280]{0:T(1024)S(1)}, f32[1280]{0:T(1024)}, u32[]{:S(2)}) copy-start(f32[1280]{0:T(1024)} %param.21) | copy-start | bytes 15364
  37.9 39.0 %copy-start.3 = (f32[1280]{0:T(1024)S(1)}, f32[1280]{0:T(1024)}, u32[]{:S(2)}) copy-start(f32[1280]{0:T(1024)} %param.22) | copy-start | bytes 15364
  38.0 88.3 %all-gather.3.cloned.1.call-start = ((), (), s32[]{:S(2)}) async-start(), calls=%async_computation.8 | async-start | bytes 3276800 | tf_op jit(solution)/shard_map/all_gather | solution.py:371
  78.6 23.9 %copy-start.5 = (f32[1280]{0:T(1024)S(1)}, f32[1280]{0:T(1024)}, u32[]{:S(2)}) copy-start(f32[1280]{0:T(1024)} %param.24) | copy-start | bytes 15364
  78.6 24.5 %copy-start.7 = (s32[1,256]{1,0:T(1,128)S(1)}, s32[1,256]{1,0:T(1,128)}, u32[]{:S(2)}) copy-start(s32[1,256]{1,0:T(1,128)} %param.16) | copy-start | bytes 3076
  102.4 178.8 %reduce-scatter.5.cloned.1.call-start = ((), (), s32[]{:S(2)}) async-start(), calls=%async_computation.7 | async-start | bytes 5242880 | tf_op jit(solution)/shard_map/reduce_scatter | solution.py:374
  238.7 43.8 %all-to-all-start = ((s32[4,1,64]{2,1,0:T(1,128)}), s32[4,1,64]{2,1,0:T(1,128)S(1)}, u32[]{:S(2)}, u32[]{:S(2)}) async-start(s32[4,1,64]{2,1,0:T(1,128)} %all_to_all.31), calls=%async_computation | async-start | bytes 4096 | tf_op jit(solution)/shard_map/all_to_all | solution.py:357
  312.6 19.4 %copy-start.4 = (f32[2048]{0:T(1024)S(1)}, f32[2048]{0:T(1024)}, u32[]{:S(2)}) copy-start(f32[2048]{0:T(1024)} %param.26) | copy-start | bytes 24580
  312.6 18.1 %all-to-all-start.3 = ((bf16[4,1,256,512]{3,2,1,0:T(8,128)(2,1)}), bf16[4,1,256,512]{3,2,1,0:T(8,128)(2,1)S(1)}, u32[]{:S(2)}, u32[]{:S(2)}) async-start(bf16[4,1,256,512]{3,2,1,0:T(8,128)(2,1)} %bitcast.53), calls=%async_computation.5 | async-start | bytes 2097152 | tf_op jit(solution)/shard_map/all_to_all | solution.py:380
Sparse Core Ops, SparseCore 0:
  38.1 37.1 reduce-scatter.2
  102.5 23.6 all-gather.2
  238.0 43.1 reduce-scatter.4

commit v3 on v2

--- a/solution.py
+++ b/solution.py
@@ -327,6 +327,153 @@
             collective_id=0, has_side_effects=True, vmem_limit_bytes=60 * 1024 * 1024
         ),
     )(x, w1, bias.reshape(chunks, 1, wide), permute, w2)
+
+
+def place_kernel(
+    n, y, out, half, across_sum, from_across, ready, landed, got,
+    mate_send, mate_recv, across_send, across_recv, row_send, row_recv, end_send, end_recv,
+):
+    quarter = y.shape[3] // 4
+    row, me = lax.axis_index("dp"), lax.axis_index("tensor")
+    core, side = me % 2, me // 2
+    mate, across = side * 2 + 1 - core, (1 - side) * 2 + core
+
+    barrier = pltpu.get_barrier_semaphore()
+    for k in range(1, 4):
+        pl.semaphore_signal(barrier, inc=1, device_id={"tensor": (me + k) % 4}, device_id_type=MESH)
+    for k in range(1, n):
+        pl.semaphore_signal(barrier, inc=1, device_id={"dp": (row + k) % n}, device_id_type=MESH)
+    pl.semaphore_wait(barrier, 3 + n - 1)
+
+    def piece(index):
+        return pl.ds(pl.multiple_of(index * quarter, quarter), quarter)
+
+    def to_mate(i, j):
+        return pltpu.make_async_remote_copy(
+            y.at[i, :, :, piece((side + j) % 2 * 2 + 1 - core)], half.at[i, j], mate_send.at[i, j], mate_recv.at[i, j],
+            device_id={"tensor": mate}, device_id_type=MESH)
+
+    def to_across(i):
+        return pltpu.make_async_remote_copy(
+            across_sum.at[i], from_across.at[i], across_send.at[i], across_recv.at[i],
+            device_id={"tensor": across}, device_id_type=MESH)
+
+    def to_row(i, k):
+        other = (row + k) % n
+        return pltpu.make_async_remote_copy(
+            ready.at[i, other], landed.at[row, i], row_send.at[i, k], row_recv.at[i, k],
+            device_id={"dp": other}, device_id_type=MESH)
+
+    def to_end(i, k, block):
+        return pltpu.make_async_remote_copy(
+            landed.at[block, i], got.at[me, i], end_send.at[i, k], end_recv.at[i, me],
+            device_id={"tensor": block}, device_id_type=MESH)
+
+    for i in range(n):
+        for j in (1, 0):
+            to_mate(i, j).start()
+
+    for i in range(n):
+        to_mate(i, 1).wait_recv()
+        for s in range(n):
+            across_sum[i, s] = (
+                y[i, s, :, piece((1 - side) * 2 + core)].astype(jnp.float32) + half[i, 1, s].astype(jnp.float32)
+            ).astype(jnp.bfloat16)
+        to_across(i).start()
+
+    for i in range(n):
+        to_mate(i, 0).wait_recv()
+        to_across(i).wait_recv()
+        for s in range(n):
+            ready[i, s] = (
+                y[i, s, :, piece(me)].astype(jnp.float32)
+                + half[i, 0, s].astype(jnp.float32)
+                + from_across[i, s].astype(jnp.float32)
+            ).astype(jnp.bfloat16)
+        for k in range(1, n):
+            to_row(i, k).start()
+        landed[row, i] = ready[i, row]
+
+    for i in range(n):
+        for k in range(n):
+            block = (row + n - k) % n
+            if k:
+                to_row(i, k).wait_recv()
+
+            @pl.when(block == me)
+            def _():
+                got[me, i] = landed[block, i]
+
+            @pl.when(block != me)
+            def _():
+                to_end(i, k, block).start()
+
+    for i in range(n):
+        for k in range(1, 4):
+            other = (me + k) % 4
+            pltpu.make_async_remote_copy(
+                landed.at[0, i], got.at[other, i], end_send.at[i, 0], end_recv.at[i, other],
+                device_id={"tensor": other}, device_id_type=MESH).wait_recv()
+    for t in range(4):
+        out[:, :, t * quarter:(t + 1) * quarter] = got[t]
+
+    for i in range(n):
+        for j in range(2):
+            to_mate(i, j).wait_send()
+        to_across(i).wait_send()
+        for k in range(1, n):
+            to_row(i, k).wait_send()
+        for k in range(n):
+            block = (row + n - k) % n
+
+            @pl.when(block != me)
+            def _():
+                to_end(i, k, block).wait_send()
+
+
+def place(second):
+    n, _, capacity, columns = second.shape
+    quarter = columns // 4
+    vmem = pl.BlockSpec(memory_space=pltpu.VMEM)
+    stack = pltpu.VMEM((n, n, capacity, quarter), jnp.bfloat16)
+    return pl.pallas_call(
+        functools.partial(place_kernel, n),
+        out_shape=jax.ShapeDtypeStruct((n, capacity, columns), jnp.bfloat16),
+        in_specs=[vmem],
+        out_specs=vmem,
+        scratch_shapes=[
+            pltpu.VMEM((n, 2, n, capacity, quarter), jnp.bfloat16),
+            stack,
+            stack,
+            stack,
+            stack,
+            stack,
+            pltpu.SemaphoreType.DMA((n, 2)),
+            pltpu.SemaphoreType.DMA((n, 2)),
+            pltpu.SemaphoreType.DMA((n,)),
+            pltpu.SemaphoreType.DMA((n,)),
+            pltpu.SemaphoreType.DMA((n, n)),
+            pltpu.SemaphoreType.DMA((n, n)),
+            pltpu.SemaphoreType.DMA((n, n)),
+            pltpu.SemaphoreType.DMA((n, n)),
+        ],
+        compiler_params=pltpu.CompilerParams(
+            collective_id=1, has_side_effects=True, vmem_limit_bytes=40 * 1024 * 1024
+        ),
+    )(second)
+
+
+def exchange(second, dp_count, tensor_count, capacity):
+    if dp_count == tensor_count == 4 and capacity % 16 == 0 and second.shape[1] % 512 == 0:
+        return place(second.reshape(dp_count, dp_count, capacity, -1)).reshape(dp_count * capacity, -1)
+    second = lax.psum_scatter(second, "tensor", scatter_dimension=1, tiled=True)
+    columns = second.shape[1]
+    second = second.reshape(dp_count, dp_count, capacity, columns)
+    second = lax.all_to_all(second, "dp", split_axis=1, concat_axis=0, tiled=False)
+    blocks = dp_count // tensor_count
+    second = second.reshape(tensor_count, blocks, dp_count * capacity, columns)
+    second = lax.all_to_all(second, "tensor", split_axis=0, concat_axis=0, tiled=True)
+    return second.transpose(2, 1, 0, 3).reshape(dp_count * capacity, -1)
 
 
 def local(
@@ -371,14 +518,7 @@
     received = lax.all_gather(sliced, "tensor", axis=1, tiled=False)
     received = received.reshape(-1, 4 * width // dp_count)
     second = merger(received, w_first, b_first, permute, w_second)
-    second = lax.psum_scatter(second, "tensor", scatter_dimension=1, tiled=True)
-    columns = second.shape[1]
-    second = second.reshape(dp_count, dp_count, capacity, columns)
-    second = lax.all_to_all(second, "dp", split_axis=1, concat_axis=0, tiled=False)
-    blocks = dp_count // tensor_count
-    second = second.reshape(tensor_count, blocks, dp_count * capacity, columns)
-    second = lax.all_to_all(second, "tensor", split_axis=0, concat_axis=0, tiled=True)
-    visual = second.transpose(2, 1, 0, 3).reshape(dp_count * capacity, -1)
+    visual = exchange(second, dp_count, tensor_count, capacity)
     visual = (visual.astype(jnp.float32) + b_second).astype(jnp.bfloat16)
     hit = jnp.arange(seq_rows, dtype=jnp.int32)[:, None] == arrived_rows[None, :]
     placed = jnp.dot(hit.astype(jnp.bfloat16), visual, preferred_element_type=jnp.float32).astype(jnp.bfloat16)

time: 344 us -> 289 us (0.84)
  waiting for transfers between devices: 112 us -> 54.3 us
  Pallas kernels: 108 us -> 148 us
  blocking collectives: 51.7 us -> 21.6 us
  starting transfers between devices: 6.99 us -> 3.21 us
    pallas_call x0 -> x1, Pallas kernels: none -> 39.8 us  [place(): pl.pallas_call(functools.partial(place_kernel, n), out_shape=jax.ShapeDty...]
    reduce_scatter x1 -> x0, waiting for transfers between devices: 39.2 us -> none  [local(): second = lax.psum_scatter(second, 'tensor', scatter_dimension=1, tiled=True)]
    all_to_all x1 -> x0, blocking collectives: 30.1 us -> none  [local(): lax.all_to_all(second, 'dp', split_axis=1, concat_axis=0, tiled=False)]
    all_to_all x1 -> x0, waiting for transfers between devices: 13 us -> none  [local(): lax.all_to_all(second, 'tensor', split_axis=0, concat_axis=0, tiled=True)]
    all_gather x1, waiting for transfers between devices: 22.2 us -> 12.7 us  [local(): received = lax.all_gather(sliced, 'tensor', axis=1, tiled=False)]
    all_to_all x1, waiting for transfers between devices: 0.01 us -> 4.25 us  [local(): lax.all_to_all(slot_rows.reshape(dp_count, capacity), 'dp', split_axis=0,...]
    all_to_all x1 -> x0, starting transfers between devices: 3.65 us -> none  [local(): lax.all_to_all(second, 'tensor', split_axis=0, concat_axis=0, tiled=True)]
  transfers between devices with their start and end apart: 5 -> 3, of which waited for: 4 -> 3; matrix products, arithmetic and copies ran while one was open for 1% -> 1% of each run, Pallas kernels for 0% -> 0%
where the time goes in v3:
time: 289 us; the launch traced here: 288 us
  Pallas kernels  148 us (51%)
  waiting for transfers between devices  54.3 us (19%)
  matrix products  26 us (9%)
  blocking collectives  21.6 us (7%)
  between operations  14.9 us (5%)
  local copies, waits for them, and re-layouts  12.5 us (4%)
  other arithmetic  7.39 us (3%)
  starting transfers between devices  3.21 us (1%)
    pallas_call x1, Pallas kernels, merger(): pl.pallas_call(functools.partial(merger_kernel, n), out_shape=jax.ShapeDt...  108 us
    pallas_call x1, Pallas kernels, place(): pl.pallas_call(functools.partial(place_kernel, n), out_shape=jax.ShapeDty...  39.8 us
    reduce_scatter x1, waiting for transfers between devices, local(): lax.psum_scatter(partial_value, 'tensor', scatter_dimension=0, tiled=True)  37.3 us
    all_to_all x1, blocking collectives, local(): lax.all_to_all(merged_in.reshape(part // 4, dp_count, 4 * width // dp_cou...  21.6 us
    all_gather x1, waiting for transfers between devices, local(): received = lax.all_gather(sliced, 'tensor', axis=1, tiled=False)  12.7 us
    sub x1, matrix products, attention(): exponent = jnp.exp(scores - peak_score)  10.9 us
    dot_general x1, matrix products, attention(): jnp.einsum('ihqk,ikhd->iqhd', weights, projected[2], preferred_element_ty...  7.43 us
  transfers between devices with their start and end apart: 3, of which 3 were waited for; matrix products, arithmetic and copies ran while one was open for 1% of the time, Pallas kernels for 0%

profile of v3, /device:TPU:0, one launch (start us, length us, event | category | flops | bytes accessed | tf_op | source)
XLA Modules:
  0.0 287.7 jit_solution(2297866779915644670)
XLA Ops:
  6.6 1.5 fusion.32
  8.0 2.4 fusion.6
  10.5 2.8 fusion.16
  13.3 1.3 fusion.31
  15.8 10.9 %fusion.33 = (f32[4,1024]{1,0:T(4,128)S(1)}, f32[4,1024,1024]{1,2,0:T(8,128)}) fusion(pred[1024]{0:T(1024)(128)(4,1)S(1)} %iota_compare_fusion.4, bf16[1024,4,80]{0,2,1:T(8,128)(2,1)} %bitcast.46, bf16[1024,4,80]{0,2,1:T(8,128)(2,1)} %bitcast.45), kind=kOutput, calls=%fused_computation.56 | convolution fusion | flops 687866880 | bytes 18105344 | tf_op jit(solution)/shard_map/sub | solution.py:50
  26.7 7.4 %fusion.21 = bf16[4,80,1024]{2,1,0:T(8,128)(2,1)S(1)} fusion(bf16[1024,4,80]{0,2,1:T(8,128)(2,1)S(1)} %bitcast.44, f32[4,1024,1024]{1,2,0:T(8,128)} %get-tuple-element.14, f32[4,1024]{1,0:T(4,128)S(1)} %get-tuple-element.13), kind=kOutput, calls=%fused_computation.26 | convolution fusion | flops 679804928 | bytes 18104320 | tf_op jit(solution)/shard_map/ihqk,ikhd->iqhd/dot_general | solution.py:52
  34.2 3.1 %convolution_convert_fusion = bf16[1024,1280]{1,0:T(8,128)(2,1)} fusion(bf16[1024,320]{0,1:T(8,128)(2,1)S(1)} %bitcast.53, bf16[320,1280]{1,0:T(8,128)(2,1)S(1)} %copy-done.8), kind=kOutput, calls=%fused_computation.15 | convolution fusion | flops 840171520 | bytes 4096000 | tf_op jit(solution)/shard_map/dot_general | solution.py:509
  37.3 37.3 %reduce-scatter.2.cloned.1.call-done = bf16[256,1280]{1,0:T(8,128)(2,1)} async-done(((bf16[1024,1280]{1,0:T(8,128)(2,1)}), bf16[256,1280]{1,0:T(8,128)(2,1)}) %reduce-scatter.2.cloned.1.call-update) | async-done | bytes 655376 | tf_op jit(solution)/shard_map/reduce_scatter | solution.py:510
  74.6 1.6 multiply_reduce_fusion
  76.3 1.6 multiply_convert_fusion
  77.9 1.0 broadcast_in_dim_reshape_reshape.3
  78.9 1.2 copy.25
  80.0 21.6 %all_to_all.24 = bf16[1,64,4,1280]{3,1,0,2:T(8,128)(2,1)} all-to-all(bf16[1,64,4,1280]{3,1,0,2:T(8,128)(2,1)S(1)} %copy.25), channel_id=1, replica_groups=mesh['groups'=2,'dp'=4,'tensor'=4] {'dp'}, dimensions={2} | all-to-all | bytes 1310720 | tf_op jit(solution)/shard_map/all_to_all | solution.py:515
  102.1 0.6 all_to_all.17
  102.7 3.2 %all-to-all-start = ((s32[4,1,64]{2,1,0:T(1,128)}), s32[4,1,64]{2,1,0:T(1,128)S(1)}, u32[]{:S(2)}, u32[]{:S(2)}) async-start(s32[4,1,64]{2,1,0:T(1,128)} %all_to_all.17), calls=%async_computation | async-start | bytes 4096 | tf_op jit(solution)/shard_map/all_to_all | solution.py:504
  105.9 0.7 fusion.25.permute
  106.6 0.6 reshape.163.bias
  107.2 4.2 %all-to-all-done = s32[4,1,64]{2,1,0:T(1,128)S(1)} async-done(((s32[4,1,64]{2,1,0:T(1,128)}), s32[4,1,64]{2,1,0:T(1,128)S(1)}, u32[]{:S(2)}, u32[]{:S(2)}) %all-to-all-start) | async-done | bytes 1056 | tf_op jit(solution)/shard_map/all_to_all | solution.py:504
  112.8 12.7 %all-gather.3.cloned.1.call-done = bf16[4,4,64,1,1280]{4,2,3,0,1:T(8,128)(2,1)} async-done(((bf16[4,1,64,1,1280]{4,2,3,0,1:T(8,128)(2,1)}), bf16[4,4,64,1,1280]{4,2,3,0,1:T(8,128)(2,1)}) %all-gather.3.cloned.1.call-update) | async-done | bytes 2621456 | tf_op jit(solution)/shard_map/all_gather | solution.py:518
  125.5 3.5 %copy.27 = bf16[4,4,64,1,1280]{4,2,1,0,3:T(8,128)(2,1)} copy(bf16[4,4,64,1,1280]{4,2,3,0,1:T(8,128)(2,1)} %all-gather.3.cloned.1.call-done) | data formatting | bytes 5242880 | tf_op jit(solution)/shard_map/all_gather | solution.py:518
  129.0 108.1 %shard_map.136 = bf16[1024,2048]{1,0:T(8,128)(2,1)} custom-call(bf16[1024,1280]{1,0:T(8,128)(2,1)} %bitcast.42, bf16[1280,1280]{1,0:T(8,128)(2,1)} %w1_hbm.1, f32[5,1,256]{2,1,0:T(1,128)} %reshape.163.bias, bf16[256,256]{1,0:T(8,128)(2,1)} %fusion.25.permute, bf16[1280,2048]{1,0:T(8,128)(2,1)} %w2_hbm.1), custom_call_target="tpu_custom_call" | custom-call | tf_op jit(solution)/shard_map/pallas_call | solution.py:304
  237.1 2.2 copy-done.1
  239.3 39.8 %shard_map.137 = bf16[4,64,2048]{2,1,0:T(8,128)(2,1)S(1)} custom-call(bf16[4,4,64,2048]{3,2,1,0:T(8,128)(2,1)S(1)} %bitcast.40), custom_call_target="tpu_custom_call" | custom-call | tf_op jit(solution)/shard_map/pallas_call | solution.py:439
  279.1 1.8 fusion.14
  (40 shorter events, 1.8 us)
Async XLA Ops:
  6.5 3.9 %copy-start = (bf16[3,1280,320]{1,2,0:T(8,128)(2,1)S(1)}, bf16[3,1280,320]{1,2,0:T(8,128)(2,1)}, u32[]{:S(2)}) copy-start(bf16[3,1280,320]{1,2,0:T(8,128)(2,1)} %param.18) | copy-start | bytes 7372804
  6.5 3.9 %copy-start.11 = (f32[3,320]{1,0:T(4,128)S(1)}, f32[3,320]{1,0:T(4,128)}, u32[]{:S(2)}) copy-start(f32[3,320]{1,0:T(4,128)} %param.19) | copy-start | bytes 11524
  6.5 3.9 %copy-start.9 = (f32[1280]{0:T(1024)S(1)}, f32[1280]{0:T(1024)}, u32[]{:S(2)}) copy-start(f32[1280]{0:T(1024)} %param.17) | copy-start | bytes 15364
  6.5 68.1 %reduce-scatter.2.cloned.1.call-start = ((), (), s32[]{:S(2)}) async-start(), calls=%async_computation.3 | async-start | bytes 3276800 | tf_op jit(solution)/shard_map/reduce_scatter | solution.py:510
  6.5 3.9 %copy-start.2 = (bf16[1024,1280]{1,0:T(8,128)(2,1)S(1)}, bf16[1024,1280]{1,0:T(8,128)(2,1)}, u32[]{:S(2)}) copy-start(bf16[1024,1280]{1,0:T(8,128)(2,1)} %param.14) | copy-start | bytes 7864324
  26.7 7.4 %copy-start.8 = (bf16[320,1280]{1,0:T(8,128)(2,1)S(1)}, bf16[320,1280]{1,0:T(8,128)(2,1)}, u32[]{:S(2)}) copy-start(bf16[320,1280]{1,0:T(8,128)(2,1)} %param.20) | copy-start | bytes 2457604
  37.2 37.4 %copy-start.3 = (f32[1280]{0:T(1024)S(1)}, f32[1280]{0:T(1024)}, u32[]{:S(2)}) copy-start(f32[1280]{0:T(1024)} %param.21) | copy-start | bytes 15364
  37.2 39.0 %copy-start.4 = (f32[1280]{0:T(1024)S(1)}, f32[1280]{0:T(1024)}, u32[]{:S(2)}) copy-start(f32[1280]{0:T(1024)} %param.22) | copy-start | bytes 15364
  37.3 88.2 %all-gather.3.cloned.1.call-start = ((), (), s32[]{:S(2)}) async-start(), calls=%async_computation.4 | async-start | bytes 3276800 | tf_op jit(solution)/shard_map/all_gather | solution.py:518
  77.9 23.8 %copy-start.6 = (s32[1,256]{1,0:T(1,128)S(1)}, s32[1,256]{1,0:T(1,128)}, u32[]{:S(2)}) copy-start(s32[1,256]{1,0:T(1,128)} %param.16) | copy-start | bytes 3076
  77.9 28.7 %copy-start.5 = (f32[1280]{0:T(1024)S(1)}, f32[1280]{0:T(1024)}, u32[]{:S(2)}) copy-start(f32[1280]{0:T(1024)} %param.24) | copy-start | bytes 15364
  102.7 8.7 %all-to-all-start = ((s32[4,1,64]{2,1,0:T(1,128)}), s32[4,1,64]{2,1,0:T(1,128)S(1)}, u32[]{:S(2)}, u32[]{:S(2)}) async-start(s32[4,1,64]{2,1,0:T(1,128)} %all_to_all.17), calls=%async_computation | async-start | bytes 4096 | tf_op jit(solution)/shard_map/all_to_all | solution.py:504
  237.1 2.2 copy-start.1
  239.3 39.8 %copy-start.7 = (bf16[384,2048]{1,0:T(8,128)(2,1)S(1)}, bf16[384,2048]{1,0:T(8,128)(2,1)}, u32[]{:S(2)}) copy-start(bf16[384,2048]{1,0:T(8,128)(2,1)} %param.27) | copy-start | bytes 4718596
  239.3 39.8 %copy-start.10 = (f32[2048]{0:T(1024)S(1)}, f32[2048]{0:T(1024)}, u32[]{:S(2)}) copy-start(f32[2048]{0:T(1024)} %param.26) | copy-start | bytes 24580
Sparse Core Ops, SparseCore 0:
  37.4 37.1 reduce-scatter.1
  101.8 23.6 all-gather.2
